TPU v7x, 128 devices: a whole 4x4x4 slice. The times are simulated.
128 devices in a mesh: seq: 16 (over z_hi, x, core), chan: 8 (over z_lo, y).
Axes of the slice: x: 4, y: 4, z: 4 (z_hi: 2, z_lo: 2; z = z_hi * 2 + z_lo), core: 2. Of those that a mesh axis runs over, the one named last changes fastest.
Arguments:
- hidden_states: bfloat16 [4096, 4096], P('chan', 'seq'), may hold values from -700 to 700
- norm_gain: float32 [4096], P('chan'), may hold values from 0.1 to 1.9
- short_filter: float32 [4096, 128], P('chan'), may hold values from -0.5 to 0.5
- long_filter: bfloat16 [4096, 4096], P('chan', 'seq'), may hold values from -0.09375 to 0.09375
- long_bias: float32 [4096], P('chan'), may hold values from -4 to 4
- gate_stream: bfloat16 [4096, 4096], P('chan', 'seq'), may hold values from -6 to 6
- upstream: bfloat16 [4096, 4096], P(None, 'seq'), may hold values from -6 to 6
Outputs:
- mixed: bfloat16 [4096, 4096], P('chan', 'seq')
- weight_grad: float32 [4096, 4096], P('seq', 'chan')
All inputs are finite; a program needn't handle non-finite values.
Results may differ from a plain program's by a relative error of at most 0.015.
Values may be sent and summed in bfloat16 or wider, within the bound.
No kernel may reach another device: no remote copies, remote signals or barrier semaphores. Data moves between devices by JAX's collectives and lax.ppermute only.
A program may use at most 64 MiB of HBM per device.

v0:
```python
import math
import jax
import jax.numpy as jnp
from jax import lax
from jax.sharding import PartitionSpec as P

D = 4096
EPSILON = 1e-05


def copy_for_each(value, axis):
    copies = jnp.broadcast_to(value, (lax.axis_size(axis), *value.shape))
    return lax.all_to_all(copies, axis, split_axis=0, concat_axis=0, tiled=True)


def over_copies(value, axis):
    everything = copy_for_each(value, axis)
    return jnp.sum(everything, axis=0)


def passed_along(value, axis, by):
    devices = lax.axis_size(axis)
    pairs = [(i, i + by) for i in range(devices) if 0 <= i + by < devices]
    return lax.ppermute(value, axis, pairs)


def short_conv(padded, taps):
    kernel = taps[:, ::-1][:, None, :]
    result = lax.conv_general_dilated(
        padded[None],
        kernel,
        (1,),
        "VALID",
        dimension_numbers=("NCH", "OIH", "NCH"),
        feature_group_count=padded.shape[0],
        precision=lax.Precision.HIGHEST,
    )
    return result[0]


def twiddle(row_total, col_total, modulus, direction):
    product = (
        jnp.arange(row_total, dtype=jnp.int32)[:, None]
        * jnp.arange(col_total, dtype=jnp.int32)[None, :]
        % modulus
    )
    angles = direction * 2.0 * math.pi * product.astype(jnp.float32) / modulus
    return (jnp.cos(angles), jnp.sin(angles))


def product_einsum(form, left, right):
    return jnp.einsum(form, left, right, precision=lax.Precision.HIGHEST)


def split_table(table):
    upper = table.astype(jnp.bfloat16)
    lower = (table - upper.astype(jnp.float32)).astype(jnp.bfloat16)
    return (upper, lower)


def table_product(table, grid):
    upper, lower = split_table(table)
    first = jnp.einsum("kn,cnm->ckm", upper, grid, preferred_element_type=jnp.float32)
    return first + jnp.einsum("kn,cnm->ckm", lower, grid, preferred_element_type=jnp.float32)


def forward_real(signal, factor_a, factor_b):
    length = factor_a * factor_b
    seq_total = signal.shape[1]
    kept_in = -(-seq_total // factor_b)
    filled = jnp.pad(signal, ((0, 0), (0, kept_in * factor_b - seq_total)))
    grid = filled.reshape(signal.shape[0], kept_in, factor_b)
    outer_re, outer_im = twiddle(factor_a, kept_in, factor_a, -1.0)
    section_re = table_product(outer_re, grid)
    section_im = table_product(outer_im, grid)
    turn_re, turn_im = twiddle(factor_a, factor_b, length, -1.0)
    rotated_re = section_re * turn_re - section_im * turn_im
    rotated_im = section_re * turn_im + section_im * turn_re
    inner_re, inner_im = twiddle(factor_b, factor_b, factor_b, -1.0)
    result_re = product_einsum("ckm,jm->ckj", rotated_re, inner_re) - product_einsum(
        "ckm,jm->ckj", rotated_im, inner_im
    )
    result_im = product_einsum("ckm,jm->ckj", rotated_re, inner_im) + product_einsum(
        "ckm,jm->ckj", rotated_im, inner_re
    )
    return (result_re, result_im)


def inverse_real(spec_re, spec_im, factor_a, factor_b, kept_rows):
    length = factor_a * factor_b
    inner_re, inner_im = twiddle(factor_b, factor_b, factor_b, 1.0)
    section_re = product_einsum("ckj,mj->ckm", spec_re, inner_re) - product_einsum(
        "ckj,mj->ckm", spec_im, inner_im
    )
    section_im = product_einsum("ckj,mj->ckm", spec_re, inner_im) + product_einsum(
        "ckj,mj->ckm", spec_im, inner_re
    )
    turn_re, turn_im = twiddle(factor_a, factor_b, length, 1.0)
    rotated_re = section_re * turn_re - section_im * turn_im
    rotated_im = section_re * turn_im + section_im * turn_re
    outer_re, outer_im = twiddle(kept_rows, factor_a, factor_a, 1.0)
    result = product_einsum("nk,ckm->cnm", outer_re, rotated_re) - product_einsum(
        "nk,ckm->cnm", outer_im, rotated_im
    )
    return result.reshape(result.shape[0], kept_rows * factor_b) / length


def long_convolution(signal, filt):
    seq_total = signal.shape[1]
    length = 2 * seq_total
    factor_a = 1
    for divisor in range(1, math.isqrt(length) + 1):
        if length % divisor == 0:
            factor_a = divisor
    factor_b = length // factor_a
    signal_re, signal_im = forward_real(signal, factor_a, factor_b)
    filter_re, filter_im = forward_real(filt, factor_a, factor_b)
    joint_re = signal_re * filter_re - signal_im * filter_im
    joint_im = signal_re * filter_im + signal_im * filter_re
    kept_rows = -(-seq_total // factor_b)
    return inverse_real(joint_re, joint_im, factor_a, factor_b, kept_rows)[:, :seq_total]


def shards(hidden_states, norm_gain, short_filter, long_filter, long_bias, gate_stream, upstream):
    states = hidden_states.astype(jnp.float32)
    partial_squares = jnp.sum(states * states, axis=0)
    squares = over_copies(partial_squares, "chan")
    normed = (states * lax.rsqrt(squares / D + EPSILON)[None, :] * norm_gain[:, None]).astype(
        jnp.bfloat16
    )
    tap_count = short_filter.shape[1]
    width_local = hidden_states.shape[0] // lax.axis_size("seq")
    owner_index = lax.axis_index("seq")
    bias_slice = lax.dynamic_slice_in_dim(long_bias, owner_index * width_local, width_local)
    tail_cols = normed[:, normed.shape[1] - tap_count :]
    from_left = passed_along(tail_cols, "seq", 1)
    padded = jnp.concatenate(
        [from_left[:, 1:].astype(jnp.float32), normed.astype(jnp.float32)], axis=1
    )
    short_out = short_conv(padded, short_filter).astype(jnp.bfloat16)
    short_whole, filter_whole = (
        lax.all_to_all(short_out, "seq", split_axis=0, concat_axis=1, tiled=True),
        lax.all_to_all(long_filter, "seq", split_axis=0, concat_axis=1, tiled=True),
    )
    long_conv = long_convolution(short_whole, filter_whole)
    long_whole = (long_conv + bias_slice[:, None] * short_whole.astype(jnp.float32)).astype(
        jnp.bfloat16
    )
    long_out = lax.all_to_all(long_whole, "seq", split_axis=1, concat_axis=0, tiled=True)
    mixed = (gate_stream.astype(jnp.float32) * long_out.astype(jnp.float32)).astype(jnp.bfloat16)
    mixed_whole = lax.all_gather(mixed, "seq", axis=1, tiled=True)
    owned = lax.all_to_all(upstream, "seq", split_axis=0, concat_axis=1, tiled=True)
    weight_grad = lax.dot_general(
        owned, mixed_whole, (((1,), (1,)), ((), ())), preferred_element_type=jnp.float32
    )
    return (mixed, weight_grad)


def solution(mesh):
    placed = (
        P("chan", "seq"),
        P("chan"),
        P("chan", None),
        P("chan", "seq"),
        P("chan"),
        P("chan", "seq"),
        P(None, "seq"),
    )
    return jax.shard_map(
        shards,
        mesh=mesh,
        in_specs=placed,
        out_specs=(P("chan", "seq"), P("seq", "chan")),
        check_vma=False,
    )
```

profile of v0, /device:TPU:1, one launch (start us, length us, event | category | flops | bytes accessed | tf_op | source)
XLA Modules:
  0.0 171.9 jit_solution(16711213002969897261)
XLA Ops:
  7.2 1.0 fusion.17
  8.2 11.2 %all_to_all.64 = f32[8,1,256]{2,1,0:T(1,128)S(1)} all-to-all(f32[8,1,256]{2,1,0:T(1,128)S(1)} %broadcast_in_dim.9), channel_id=1, replica_groups=mesh['seq'=16,'chan'=8] {'chan'}, dimensions={0} | all-to-all | bytes 16384 | tf_op jit(solution)/shard_map/all_to_all | solution.py:13
  19.4 9.4 %all-to-all-start.2 = ((bf16[16,32,256]{2,1,0:T(8,128)(2,1)}), bf16[16,32,256]{2,1,0:T(8,128)(2,1)S(1)}, u32[]{:S(2)}, u32[]{:S(2)}) async-start(bf16[16,32,256]{2,1,0:T(8,128)(2,1)} %bitcast.111), calls=%async_computation.2 | async-start | bytes 524288 | tf_op jit(solution)/shard_map/all_to_all | solution.py:143
  28.9 1.1 fusion.19
  30.0 3.5 %collective-permute-start = (bf16[512,128]{1,0:T(8,128)(2,1)S(1)}, bf16[512,128]{1,0:T(8,128)(2,1)S(1)}, u32[]{:S(2)}, u32[]{:S(2)}) collective-permute-start(bf16[512,128]{1,0:T(8,128)(2,1)S(1)} %slice.8), channel_id=1, source_target_pairs={{0,8},{8,16},{16,24},{24,32},{32,40},{40,48},{48,56},{56,64},{64,7... | collective-permute-start | bytes 393224 | tf_op jit(solution)/shard_map/ppermute | solution.py:24
  33.7 1.9 %rev.3 = f32[512,128]{1,0:T(8,128)S(1)} reverse(f32[512,128]{1,0:T(8,128)} %param.9), dimensions={1} | reverse | bytes 524288 | tf_op jit(solution)/shard_map/rev | solution.py:28
  37.0 1.1 copy.48
  38.2 8.4 %convolution_convert_fusion = bf16[1,512,256]{1,0,2:T(2,128)(2,1)S(1)} fusion(bf16[1,512,383]{1,0,2:T(2,128)(2,1)S(1)} %copy.48, f32[512,1,128]{0,1,2:T(1,128)S(1)} %copy.49), kind=kOutput, calls=%fused_computation.12 | convolution fusion | flops 201457664 | bytes 916480 | tf_op jit(solution)/shard_map/conv_general_dilated | solution.py:29
  46.6 1.1 copy.50
  47.7 8.0 %all-to-all-start.1 = ((bf16[16,32,256]{2,1,0:T(8,128)(2,1)}), bf16[16,32,256]{2,1,0:T(8,128)(2,1)S(1)}, u32[]{:S(2)}, u32[]{:S(2)}) async-start(bf16[16,32,256]{2,1,0:T(8,128)(2,1)} %bitcast.2), calls=%async_computation.1 | async-start | bytes 524288 | tf_op jit(solution)/shard_map/all_to_all | solution.py:142
  57.9 1.2 fusion.6
  59.1 1.2 fusion.8
  60.3 1.2 convolution_add_fusion.1
  61.6 1.2 convolution_subtract_fusion.1
  62.9 1.6 all-to-all-done.1
  66.4 1.2 fusion.27
  67.6 1.3 fusion.26
  68.9 1.3 convolution_subtract_fusion.2
  70.2 1.7 %multiply_add_fusion = (f32[32,64,128]{2,1,0:T(8,128)S(1)}, f32[32,64,128]{2,1,0:T(8,128)S(1)}) fusion(f32[32,64,128]{2,1,0:T(8,128)S(1)} %convolution_subtract_fusion.1, f32[32,64,128]{2,1,0:T(8,128)S(1)} %convolution_subtract_fusion.2, f32[32,64,128]{2,1,0:T(8,128)S(1)} %convolution_add_fusion.1, f32[32,64,128]{2,1,0:T(8,128)S(1)} %fusion.26, ...), kind=kOutput, calls=%fused_computation.30 | convolution fusion | flops 405504000 | bytes 8454144 | tf_op jit(solution)/shard_map/ckm,jm->ckj/dot_general | solution.py:52
  71.9 1.2 fusion.34
  73.2 1.2 fusion.30
  74.4 1.3 convolution_subtract_fusion
  75.7 1.2 convolution_add_fusion
  76.9 0.9 fusion.13
  77.8 0.9 fusion.3
  79.2 14.1 %all_to_all.65 = bf16[32,16,256]{2,0,1:T(8,128)(2,1)S(1)} all-to-all(bf16[32,16,256]{2,0,1:T(8,128)(2,1)S(1)} %fusion.21), channel_id=1, replica_groups=mesh['seq'=16,'chan'=8] {'seq'}, dimensions={1} | all-to-all | bytes 524288 | tf_op jit(solution)/shard_map/all_to_all | solution.py:149
  93.4 0.8 fusion.20
  94.2 36.4 %all_to_all.66 = bf16[16,256,256]{2,1,0:T(8,128)(2,1)S(1)} all-to-all(bf16[16,256,256]{2,1,0:T(8,128)(2,1)} %bitcast.107), channel_id=1, replica_groups=mesh['seq'=16,'chan'=8] {'seq'}, dimensions={0} | all-to-all | bytes 4194304 | tf_op jit(solution)/shard_map/all_to_all | solution.py:152
  130.6 2.4 %copy.54 = bf16[256,16,256]{0,2,1:T(8,128)(2,1)} copy(bf16[256,16,256]{2,0,1:T(8,128)(2,1)S(1)} %bitcast.105) | data formatting | bytes 4194304 | tf_op jit(solution)/shard_map/all_to_all | solution.py:152
  132.9 27.0 %all-gather.2.cloned.1.call-done = bf16[512,4096]{1,0:T(8,128)(2,1)} async-done(((bf16[512,256]{1,0:T(8,128)(2,1)}), bf16[512,4096]{1,0:T(8,128)(2,1)}) %all-gather.2.cloned.1.call-update) | async-done | bytes 4194320 | tf_op jit(solution)/shard_map/all_gather | solution.py:151
  159.9 4.1 %convolution_bitcast_fusion = f32[256,512]{0,1:T(8,128)S(1)} fusion(bf16[512,4096]{1,0:T(8,128)(2,1)} %all-gather.2.cloned.1.call-done, bf16[256,4096]{0,1:T(8,128)(2,1)} %bitcast.108), kind=kOutput, calls=%fused_computation.13 | convolution fusion | flops 1073741824 | bytes 6815744 | tf_op jit(solution)/shard_map/dot_general | solution.py:153
  164.1 1.0 copy.55
  (30 shorter events, 6.0 us)
Async XLA Ops:
  19.4 28.3 %all-to-all-start.2 = ((bf16[16,32,256]{2,1,0:T(8,128)(2,1)}), bf16[16,32,256]{2,1,0:T(8,128)(2,1)S(1)}, u32[]{:S(2)}, u32[]{:S(2)}) async-start(bf16[16,32,256]{2,1,0:T(8,128)(2,1)} %bitcast.111), calls=%async_computation.2 | async-start | bytes 524288 | tf_op jit(solution)/shard_map/all_to_all | solution.py:143
  30.0 6.7 %collective-permute-start = (bf16[512,128]{1,0:T(8,128)(2,1)S(1)}, bf16[512,128]{1,0:T(8,128)(2,1)S(1)}, u32[]{:S(2)}, u32[]{:S(2)}) collective-permute-start(bf16[512,128]{1,0:T(8,128)(2,1)S(1)} %slice.8), channel_id=1, source_target_pairs={{0,8},{8,16},{16,24},{24,32},{32,40},{40,48},{48,56},{56,64},{64,7... | collective-permute-start | bytes 393224 | tf_op jit(solution)/shard_map/ppermute | solution.py:24
  47.7 16.7 %all-to-all-start.1 = ((bf16[16,32,256]{2,1,0:T(8,128)(2,1)}), bf16[16,32,256]{2,1,0:T(8,128)(2,1)S(1)}, u32[]{:S(2)}, u32[]{:S(2)}) async-start(bf16[16,32,256]{2,1,0:T(8,128)(2,1)} %bitcast.2), calls=%async_computation.1 | async-start | bytes 524288 | tf_op jit(solution)/shard_map/all_to_all | solution.py:142
  55.8 104.2 %all-gather.2.cloned.1.call-start = ((), (), s32[]{:S(2)}) async-start(), calls=%async_computation.5 | async-start | bytes 4456448 | tf_op jit(solution)/shard_map/all_gather | solution.py:151
  78.7 14.6 %copy-start = (bf16[512,256]{1,0:T(8,128)(2,1)S(1)}, bf16[512,256]{1,0:T(8,128)(2,1)}, u32[]{:S(2)}) copy-start(bf16[512,256]{1,0:T(8,128)(2,1)} %param.12) | copy-start | bytes 786436
Sparse Core Ops, SparseCore 0:
  94.3 65.6 all-gather.1
where the time goes:
time: 173 us; the launch traced here: 172 us
  blocking collectives  61.7 us (36%)
  matrix products  33.1 us (19%)
  waiting for transfers between devices  28.6 us (17%)
  starting transfers between devices  21.2 us (12%)
  between operations  14.3 us (8%)
  local copies, waits for them, and re-layouts  9.21 us (5%)
  other arithmetic  3.75 us (2%)
    all_to_all x1, blocking collectives, shards(): lax.all_to_all(upstream, 'seq', split_axis=0, concat_axis=1, tiled=True)  36.4 us
    all_gather x1, waiting for transfers between devices, shards(): mixed_whole = lax.all_gather(mixed, 'seq', axis=1, tiled=True)  27 us
    dot_general x14, matrix products, product_einsum(): return jnp.einsum(form, left, right, precision=lax.Precision.HIGHEST)  17.2 us
    all_to_all x1, blocking collectives, shards(): lax.all_to_all(long_whole, 'seq', split_axis=1, concat_axis=0, tiled=True)  14.1 us
    all_to_all x1, blocking collectives, copy_for_each(): return lax.all_to_all(copies, axis, split_axis=0, concat_axis=0, tiled=True)  11.2 us
    all_to_all x1, starting transfers between devices, shards(): lax.all_to_all(long_filter, 'seq', split_axis=0, concat_axis=1, tiled=True)  9.44 us
    conv_general_dilated x1, matrix products, short_conv(): lax.conv_general_dilated(padded[None], kernel, (1,), 'VALID', dimension_n...  8.45 us
    all_to_all x1, starting transfers between devices, shards(): lax.all_to_all(short_out, 'seq', split_axis=0, concat_axis=1, tiled=True)  8 us
  transfers between devices with their start and end apart: 4, of which 2 were waited for; matrix products, arithmetic and copies ran while one was open for 14% of the time, Pallas kernels for 0%

commit v1 on v0

--- a/solution.py
+++ b/solution.py
@@ -148,7 +148,9 @@
     )
     long_out = lax.all_to_all(long_whole, "seq", split_axis=1, concat_axis=0, tiled=True)
     mixed = (gate_stream.astype(jnp.float32) * long_out.astype(jnp.float32)).astype(jnp.bfloat16)
-    mixed_whole = lax.all_gather(mixed, "seq", axis=1, tiled=True)
+    mixed_whole = jnp.concatenate(
+        lax.all_to_all(jnp.stack([mixed] * lax.axis_size("seq")), "seq", 0, 0), axis=1
+    )
     owned = lax.all_to_all(upstream, "seq", split_axis=0, concat_axis=1, tiled=True)
     weight_grad = lax.dot_general(
         owned, mixed_whole, (((1,), (1,)), ((), ())), preferred_element_type=jnp.float32

time: 173 us -> 178 us (1.029)
  blocking collectives: 61.7 us -> 80.5 us
  between operations: 14.3 us -> 0.95 us
  starting transfers between devices: 21.2 us -> 25.2 us
  matrix products: 33.1 us -> 29.8 us
  local copies, waits for them, and re-layouts: 9.21 us -> 7.25 us
  waiting for transfers between devices: 28.6 us -> 30.4 us
    all_to_all x0 -> x1, waiting for transfers between devices: none -> 28.5 us  [shards(): lax.all_to_all(upstream, 'seq', split_axis=0, concat_axis=1, tiled=True)]
    all_gather x1 -> x0, waiting for transfers between devices: 27 us -> none  [shards(): mixed_whole = lax.all_gather(mixed, 'seq', axis=1, tiled=True)]
    all_to_all x1, blocking collectives: 36.4 us -> 55.4 us  [shards(): lax.all_to_all(jnp.stack([mixed] * lax.axis_size('seq')), 'seq', 0, 0)]
    all_to_all x0 -> x1, starting transfers between devices: none -> 4.25 us  [shards(): lax.all_to_all(upstream, 'seq', split_axis=0, concat_axis=1, tiled=True)]
    dot_general x1, matrix products: 4.11 us -> 1.28 us  [shards(): lax.dot_general(owned, mixed_whole, (((1,), (1,)), ((), ())), preferred_e...]
    all_to_all x1 -> x0, local copies, waits for them, and re-layouts: 2.37 us -> none  [shards(): lax.all_to_all(upstream, 'seq', split_axis=0, concat_axis=1, tiled=True)]
  transfers between devices with their start and end apart: 4 -> 4, of which waited for: 2 -> 2; matrix products, arithmetic and copies ran while one was open for 14% -> 12% of each run, Pallas kernels for 0% -> 0%
where the time goes in v1:
time: 178 us; the launch traced here: 177 us
  blocking collectives  80.5 us (45%)
  waiting for transfers between devices  30.4 us (17%)
  matrix products  29.8 us (17%)
  starting transfers between devices  25.2 us (14%)
  local copies, waits for them, and re-layouts  7.25 us (4%)
  other arithmetic  3.05 us (2%)
    all_to_all x1, blocking collectives, shards(): lax.all_to_all(jnp.stack([mixed] * lax.axis_size('seq')), 'seq', 0, 0)  55.4 us
    all_to_all x1, waiting for transfers between devices, shards(): lax.all_to_all(upstream, 'seq', split_axis=0, concat_axis=1, tiled=True)  28.5 us
    dot_general x14, matrix products, product_einsum(): return jnp.einsum(form, left, right, precision=lax.Precision.HIGHEST)  17.1 us
    all_to_all x1, blocking collectives, shards(): lax.all_to_all(long_whole, 'seq', split_axis=1, concat_axis=0, tiled=True)  13.9 us
    all_to_all x1, blocking collectives, copy_for_each(): return lax.all_to_all(copies, axis, split_axis=0, concat_axis=0, tiled=True)  11.2 us
    all_to_all x1, starting transfers between devices, shards(): lax.all_to_all(long_filter, 'seq', split_axis=0, concat_axis=1, tiled=True)  9.44 us
    conv_general_dilated x1, matrix products, short_conv(): lax.conv_general_dilated(padded[None], kernel, (1,), 'VALID', dimension_n...  8.08 us
    all_to_all x1, starting transfers between devices, shards(): lax.all_to_all(short_out, 'seq', split_axis=0, concat_axis=1, tiled=True)  8 us
  transfers between devices with their start and end apart: 4, of which 2 were waited for; matrix products, arithmetic and copies ran while one was open for 12% of the time, Pallas kernels for 0%

profile of v1, /device:TPU:1, one launch (start us, length us, event | category | flops | bytes accessed | tf_op | source)
XLA Modules:
  0.0 177.1 jit_solution(10999091406086390878)
XLA Ops:
  0.6 1.0 fusion.25
  1.7 11.2 %all_to_all.66 = f32[8,1,256]{2,1,0:T(1,128)S(1)} all-to-all(f32[8,1,256]{2,1,0:T(1,128)S(1)} %broadcast_in_dim.9), channel_id=1, replica_groups=mesh['seq'=16,'chan'=8] {'chan'}, dimensions={0} | all-to-all | bytes 16384 | tf_op jit(solution)/shard_map/all_to_all | solution.py:13
  12.9 9.4 %all-to-all-start.2 = ((bf16[16,32,256]{2,1,0:T(8,128)(2,1)}), bf16[16,32,256]{2,1,0:T(8,128)(2,1)S(1)}, u32[]{:S(2)}, u32[]{:S(2)}) async-start(bf16[16,32,256]{2,1,0:T(8,128)(2,1)} %bitcast.116), calls=%async_computation.2 | async-start | bytes 524288 | tf_op jit(solution)/shard_map/all_to_all | solution.py:143
  22.4 1.1 fusion.27
  23.5 3.5 %collective-permute-start = (bf16[512,128]{1,0:T(8,128)(2,1)S(1)}, bf16[512,128]{1,0:T(8,128)(2,1)S(1)}, u32[]{:S(2)}, u32[]{:S(2)}) collective-permute-start(bf16[512,128]{1,0:T(8,128)(2,1)S(1)} %slice.8), channel_id=1, source_target_pairs={{0,8},{8,16},{16,24},{24,32},{32,40},{40,48},{48,56},{56,64},{64,7... | collective-permute-start | bytes 393224 | tf_op jit(solution)/shard_map/ppermute | solution.py:24
  27.2 1.9 %rev.3 = f32[512,128]{1,0:T(8,128)S(1)} reverse(f32[512,128]{1,0:T(8,128)} %param.9), dimensions={1} | reverse | bytes 524288 | tf_op jit(solution)/shard_map/rev | solution.py:28
  29.3 0.8 dynamic_slice.3
  30.5 1.1 copy.38
  31.6 8.1 %convolution_convert_fusion = bf16[1,512,256]{1,0,2:T(2,128)(2,1)S(1)} fusion(bf16[1,512,383]{1,0,2:T(2,128)(2,1)S(1)} %copy.38, f32[512,1,128]{0,1,2:T(1,128)S(1)} %copy.39), kind=kOutput, calls=%fused_computation.15 | convolution fusion | flops 201457664 | bytes 916480 | tf_op jit(solution)/shard_map/conv_general_dilated | solution.py:29
  39.7 1.1 copy.40
  40.8 8.0 %all-to-all-start.1 = ((bf16[16,32,256]{2,1,0:T(8,128)(2,1)}), bf16[16,32,256]{2,1,0:T(8,128)(2,1)S(1)}, u32[]{:S(2)}, u32[]{:S(2)}) async-start(bf16[16,32,256]{2,1,0:T(8,128)(2,1)} %bitcast.2), calls=%async_computation.1 | async-start | bytes 524288 | tf_op jit(solution)/shard_map/all_to_all | solution.py:142
  50.7 1.2 fusion.14
  52.0 1.2 fusion.16
  53.2 1.2 convolution_add_fusion.1
  54.5 1.2 convolution_subtract_fusion.1
  55.7 1.9 %all-to-all-done.1 = bf16[16,32,256]{2,1,0:T(8,128)(2,1)S(1)} async-done(((bf16[16,32,256]{2,1,0:T(8,128)(2,1)}), bf16[16,32,256]{2,1,0:T(8,128)(2,1)S(1)}, u32[]{:S(2)}, u32[]{:S(2)}) %all-to-all-start.1) | async-done | bytes 262176 | tf_op jit(solution)/shard_map/all_to_all | solution.py:142
  59.5 1.2 fusion.35
  60.7 1.3 fusion.34
  62.0 1.3 convolution_subtract_fusion.2
  63.3 1.7 multiply_add_fusion
  65.0 1.2 fusion.42
  66.2 1.2 fusion.38
  67.5 1.3 convolution_subtract_fusion
  68.7 1.2 convolution_add_fusion
  70.0 0.9 fusion.21
  70.9 0.9 fusion.11
  72.3 13.9 %all_to_all.67 = bf16[32,16,256]{2,0,1:T(8,128)(2,1)S(1)} all-to-all(bf16[32,16,256]{2,0,1:T(8,128)(2,1)S(1)} %fusion.29), channel_id=1, replica_groups=mesh['seq'=16,'chan'=8] {'seq'}, dimensions={1} | all-to-all | bytes 524288 | tf_op jit(solution)/shard_map/all_to_all | solution.py:149
  86.2 4.3 %all-to-all-start.5 = ((bf16[16,256,256]{2,1,0:T(8,128)(2,1)}), bf16[16,256,256]{2,1,0:T(8,128)(2,1)S(1)}, u32[]{:S(2)}, u32[]{:S(2)}) async-start(bf16[16,256,256]{2,1,0:T(8,128)(2,1)} %bitcast.24), calls=%async_computation.5 | async-start | bytes 4194304 | tf_op jit(solution)/shard_map/all_to_all | solution.py:154
  90.5 28.5 %all-to-all-done.5 = bf16[16,256,256]{2,1,0:T(8,128)(2,1)S(1)} async-done(((bf16[16,256,256]{2,1,0:T(8,128)(2,1)}), bf16[16,256,256]{2,1,0:T(8,128)(2,1)S(1)}, u32[]{:S(2)}, u32[]{:S(2)}) %all-to-all-start.5) | async-done | bytes 2097184 | tf_op jit(solution)/shard_map/all_to_all | solution.py:154
  119.4 55.4 %all_to_all.68 = bf16[16,512,256]{2,1,0:T(8,128)(2,1)S(1)} all-to-all(bf16[16,512,256]{2,1,0:T(8,128)(2,1)S(1)} %stack.2), channel_id=1, replica_groups=mesh['seq'=16,'chan'=8] {'seq'}, dimensions={0} | all-to-all | bytes 8388608 | tf_op jit(solution)/shard_map/all_to_all | solution.py:152
  174.9 1.3 fusion.5
  176.2 1.0 copy.44
  (31 shorter events, 5.5 us)
Async XLA Ops:
  12.9 28.0 %all-to-all-start.2 = ((bf16[16,32,256]{2,1,0:T(8,128)(2,1)}), bf16[16,32,256]{2,1,0:T(8,128)(2,1)S(1)}, u32[]{:S(2)}, u32[]{:S(2)}) async-start(bf16[16,32,256]{2,1,0:T(8,128)(2,1)} %bitcast.116), calls=%async_computation.2 | async-start | bytes 524288 | tf_op jit(solution)/shard_map/all_to_all | solution.py:143
  23.5 6.7 %collective-permute-start = (bf16[512,128]{1,0:T(8,128)(2,1)S(1)}, bf16[512,128]{1,0:T(8,128)(2,1)S(1)}, u32[]{:S(2)}, u32[]{:S(2)}) collective-permute-start(bf16[512,128]{1,0:T(8,128)(2,1)S(1)} %slice.8), channel_id=1, source_target_pairs={{0,8},{8,16},{16,24},{24,32},{32,40},{40,48},{48,56},{56,64},{64,7... | collective-permute-start | bytes 393224 | tf_op jit(solution)/shard_map/ppermute | solution.py:24
  40.8 16.7 %all-to-all-start.1 = ((bf16[16,32,256]{2,1,0:T(8,128)(2,1)}), bf16[16,32,256]{2,1,0:T(8,128)(2,1)S(1)}, u32[]{:S(2)}, u32[]{:S(2)}) async-start(bf16[16,32,256]{2,1,0:T(8,128)(2,1)} %bitcast.2), calls=%async_computation.1 | async-start | bytes 524288 | tf_op jit(solution)/shard_map/all_to_all | solution.py:142
  71.8 18.6 %copy-start.1 = (bf16[512,256]{1,0:T(8,128)(2,1)S(1)}, bf16[512,256]{1,0:T(8,128)(2,1)}, u32[]{:S(2)}) copy-start(bf16[512,256]{1,0:T(8,128)(2,1)} %param.12) | copy-start | bytes 786436
  86.2 32.9 %all-to-all-start.5 = ((bf16[16,256,256]{2,1,0:T(8,128)(2,1)}), bf16[16,256,256]{2,1,0:T(8,128)(2,1)S(1)}, u32[]{:S(2)}, u32[]{:S(2)}) async-start(bf16[16,256,256]{2,1,0:T(8,128)(2,1)} %bitcast.24), calls=%async_computation.5 | async-start | bytes 4194304 | tf_op jit(solution)/shard_map/all_to_all | solution.py:154
  90.5 84.4 %copy-start = (bf16[512,256]{1,0:T(8,128)(2,1)}, bf16[512,256]{1,0:T(8,128)(2,1)S(1)}, u32[]{:S(2)}) copy-start(bf16[512,256]{1,0:T(8,128)(2,1)S(1)} %fusion.28) | copy-start | bytes 786436
